TPU v7x, 512 devices: a whole 4x8x8 slice. The times are simulated.
512 devices in a mesh: seq: 32 (over x, y), chan: 8 (over z), dp: 2 (over core).
Axes of the slice: x: 4, y: 8, z: 8, core: 2. Of those that a mesh axis runs over, the one named last changes fastest.
Arguments:
- ssm_input: bfloat16 [2, 4096, 4096], P('dp', 'seq', 'chan'), may hold values from -6 to 6
- gate_z: bfloat16 [2, 4096, 4096], P('dp', 'seq', 'chan'), may hold values from -6 to 6
- b_proj: bfloat16 [2, 4096, 128], P('dp', 'seq'), may hold values from -0.52734375 to 0.52734375
- c_proj: bfloat16 [2, 4096, 128], P('dp', 'seq'), may hold values from -6 to 6
- step_size: float32 [2, 4096, 64], P('dp', 'seq', 'chan'), may hold values from 0.02 to 0.2
- log_decay: float32 [2, 4096, 64], P('dp', 'seq', 'chan'), may hold values from -1 to 0, as said below
- skip_d: float32 [64], P('chan'), may hold values from 0.5 to 1.5
- norm_gain: float32 [4096], P('chan'), may hold values from 0.5 to 1.5
- w_out: bfloat16 [4096, 2048], P('chan'), may hold values from -0.09375 to 0.09375
- d_out: bfloat16 [2, 4096, 2048], P('dp', 'seq', 'chan'), may hold values from -6 to 6
- game_lengths: int32 [2, 4], P('dp'), may hold values from 1 to 2048, 4096 in all within a row
Outputs:
- out: bfloat16 [2, 4096, 2048], P('dp', 'seq', 'chan')
- grad_x: bfloat16 [2, 4096, 4096], P('dp', 'seq', 'chan')
- grad_gain: float32 [4096], P('chan')
- grad_skip: float32 [64], P('chan')
Inputs may be any that keep to these rules, and one draw needn't show every extreme that they name: `game_lengths`: each row's 4 game lengths sum to 4096, and the longest is exactly 2048. `log_decay`: a log decay per position and head.
All inputs are finite; a program needn't handle non-finite values.
Results may differ from a plain program's by a relative error of at most 0.017.
Values may be sent and summed in bfloat16 or wider, within the bound.
A program may use at most 64 MiB of HBM per device.

v0:
```python
import jax
import jax.numpy as jnp
from jax import lax
from jax.sharding import Mesh
from jax.sharding import PartitionSpec as P

SEQ = ("seq_0", "seq_1")
SEQ_DP = ("seq_0", "seq_1", "dp")
NORM_EPS = 1e-05


def filled_with(value, identity):
    return jax.tree.map(
        lambda part, zero: jnp.zeros_like(part) + jnp.asarray(zero, part.dtype), value, identity
    )


def prefix_by_axis(value, axes, combine, identity, reverse):
    before = start = filled_with(value, identity)
    so_far = value
    for axis in reversed(axes):
        length, mine = (lax.axis_size(axis), lax.axis_index(axis))
        pieces = jax.tree.map(
            lambda part, kind: lax.all_gather(part.astype(kind), axis),
            so_far,
            (jnp.bfloat16, jnp.bfloat16),
        )
        inside, so_far = (start, start)
        for k in reversed(range(length)) if reverse else range(length):
            passed = k > mine if reverse else k < mine
            so_far = combine(
                so_far, jax.tree.map(lambda part, own: part[k].astype(own.dtype), pieces, value)
            )
            inside = jax.tree.map(lambda new, old: jnp.where(passed, new, old), so_far, inside)
        before = combine(inside, before)
    return before


def in_blocks(value, dim, length):
    lengths = value.shape
    pieces = value.reshape(*lengths[:dim], length, lengths[dim] // length, *lengths[dim + 1 :])
    return jnp.moveaxis(pieces, dim, 0)


def sent_and_summed(value, axis, dim):
    length = lax.axis_size(axis)
    pieces = lax.all_to_all(in_blocks(value, dim, length), axis, 0, 0, tiled=True)
    return jnp.sum(pieces.astype(jnp.float32), axis=0)


def copy_for_each(value, axis):
    length = lax.axis_size(axis)
    return lax.all_to_all(
        jnp.broadcast_to(value[None], (length, *value.shape)), axis, 0, 0, tiled=True
    )


def taken_together(value, axis):
    return copy_for_each(value, axis).sum(axis=0)


def block_parts(c_block, b_block, dt_block, decay_block, reset_block):
    block_len = c_block.shape[0]
    running = jnp.cumsum(decay_block, axis=0)
    reset_count = jnp.cumsum(reset_block, axis=0)
    scores = lax.dot_general(
        c_block, b_block, (((1,), (1,)), ((), ())), preferred_element_type=jnp.float32
    )
    indices = jnp.arange(block_len, dtype=jnp.int32)
    allowed = (indices[:, None] >= indices[None, :]) & (
        reset_count[:, None] == reset_count[None, :]
    )
    log_gap = running.T[:, :, None] - running.T[:, None, :]
    mixing = (
        jnp.where(allowed[None], jnp.exp(jnp.minimum(log_gap, 0.0)), 0.0)
        * scores[None]
        * dt_block.T[:, None, :]
    )
    mixing = mixing.astype(jnp.bfloat16)
    end_count = reset_count[-1]
    carry_weight = jnp.where((reset_count == 0)[:, None], jnp.exp(running), 0.0)
    tail_weight = jnp.where(
        (reset_count == end_count)[:, None], jnp.exp(running[-1][None, :] - running), 0.0
    )
    block_decay = jnp.where(end_count == 0, jnp.exp(running[-1]), 0.0)
    return (mixing, carry_weight, tail_weight, block_decay)


def chain_link(earlier, later):
    return (earlier[0] * later[0], later[0][:, None, None] * earlier[1] + later[1])


def local(
    ssm_input,
    gate_z,
    b_proj,
    c_proj,
    step_size,
    log_decay,
    skip_d,
    norm_gain,
    w_out,
    d_out,
    game_lengths,
):
    seq_len = ssm_input.shape[1]
    local_width = ssm_input.shape[2]
    heads_here = step_size.shape[2]
    head_dim = local_width // heads_here
    state_dim = b_proj.shape[2]
    block_len = min(512, seq_len)
    count_blocks = seq_len // block_len
    total_width = local_width * lax.axis_size("chan")
    x_heads = ssm_input[0].reshape(seq_len, heads_here, head_dim)
    c_rows = c_proj[0]
    b_rows = b_proj[0]
    dt_rows = step_size[0]
    lengths = game_lengths[0]
    starts = jnp.cumsum(lengths) - lengths
    sequence_positions = lax.axis_index(SEQ) * seq_len + jnp.arange(seq_len, dtype=jnp.int32)
    resets = jnp.any(sequence_positions[:, None] == starts[None, :], axis=1).astype(jnp.int32)

    def blocked(array):
        return array.reshape((count_blocks, block_len) + array.shape[1:])

    zero_state = jnp.zeros((heads_here, state_dim, head_dim), jnp.float32)
    unit_decay = jnp.ones((heads_here,), jnp.float32)

    def forward_step(state_pair, block_inputs):
        local_state, before = state_pair
        x_block, c_block, b_block, dt_block, decay_block, reset_block = block_inputs
        mixing, carry_weight, tail_weight, block_decay = block_parts(
            c_block, b_block, dt_block, decay_block, reset_block
        )
        inside = jnp.einsum("hts,shp->thp", mixing, x_block, preferred_element_type=jnp.float32)
        carried = carry_weight[:, :, None] * jnp.einsum(
            "tn,hnp->thp", c_block.astype(jnp.float32), local_state
        )
        scaled = ((tail_weight * dt_block)[:, :, None] * x_block).astype(jnp.bfloat16)
        fresh_state = jnp.einsum("sn,shp->hnp", b_block, scaled, preferred_element_type=jnp.float32)
        new_pair = (block_decay[:, None, None] * local_state + fresh_state, before * block_decay)
        return (
            new_pair,
            (
                inside + carried,
                carry_weight * before[None, :],
                mixing,
                carry_weight,
                tail_weight,
                block_decay,
            ),
        )

    forward_inputs = (
        blocked(x_heads),
        blocked(c_rows),
        blocked(b_rows),
        blocked(dt_rows),
        blocked(log_decay[0]),
        blocked(resets),
    )
    (dev_state, dev_decay), (
        ssd_blocks,
        incoming_weight,
        mixings,
        carry_weights,
        tail_weights,
        block_decays,
    ) = lax.scan(forward_step, (zero_state, unit_decay), forward_inputs)
    _, incoming = prefix_by_axis(
        (dev_decay, dev_state), SEQ, chain_link, (unit_decay, zero_state), False
    )
    from_left = jnp.einsum("tn,hnp->thp", c_rows.astype(jnp.float32), incoming)
    ssd_out = (
        ssd_blocks.reshape(seq_len, heads_here, head_dim)
        + incoming_weight.reshape(seq_len, heads_here)[:, :, None] * from_left
    )
    ssd_out = ssd_out + skip_d[None, :, None] * x_heads.astype(jnp.float32)
    gate_act = jax.nn.silu(gate_z[0].astype(jnp.float32))
    gated = ssd_out.reshape(seq_len, local_width) * gate_act
    square_total = lax.psum(jnp.sum(gated * gated, axis=1), "chan")
    inv_rms = lax.rsqrt(square_total / total_width + NORM_EPS)
    normed = (gated * norm_gain).astype(jnp.bfloat16)
    w_cols = w_out
    projected = sent_and_summed(
        lax.dot_general(
            w_cols, normed, (((0,), (1,)), ((), ())), preferred_element_type=jnp.float32
        ).astype(jnp.bfloat16),
        "chan",
        0,
    ).T
    out = (inv_rms[:, None] * projected).astype(jnp.bfloat16)[None]
    cotangent = d_out[0]
    w_cols = w_out
    pulled = lax.dot_general(
        lax.all_gather(cotangent, "chan", axis=1, tiled=True),
        w_cols,
        (((1,), (1,)), ((), ())),
        preferred_element_type=jnp.float32,
    )
    out_dot = lax.psum(jnp.sum(cotangent.astype(jnp.float32) * projected, axis=1), "chan")
    d_normed = inv_rms[:, None] * pulled
    gain_local = jnp.sum(gated * d_normed, axis=0)
    d_ssd = (
        (norm_gain * d_normed - (inv_rms**3 * out_dot / total_width)[:, None] * gated) * gate_act
    ).astype(jnp.bfloat16)
    d_heads = d_ssd.reshape(seq_len, heads_here, head_dim)
    skip_local = jnp.sum(d_heads.astype(jnp.float32) * x_heads.astype(jnp.float32), axis=(0, 2))
    grad_gain, grad_skip = (taken_together(gain_local, SEQ_DP), taken_together(skip_local, SEQ_DP))

    def backward_step(state_pair, block_inputs):
        local_adjoint, later_decay = state_pair
        d_block, c_block, b_block, dt_block, mixing, carry_weight, tail_weight, block_decay = (
            block_inputs
        )
        inside = jnp.einsum("hts,thp->shp", mixing, d_block, preferred_element_type=jnp.float32)
        carried = (dt_block * tail_weight)[:, :, None] * jnp.einsum(
            "sn,hnp->shp", b_block.astype(jnp.float32), local_adjoint
        )
        weighted = (carry_weight[:, :, None] * d_block).astype(jnp.bfloat16)
        fresh_adjoint = jnp.einsum(
            "tn,thp->hnp", c_block, weighted, preferred_element_type=jnp.float32
        )
        new_pair = (
            fresh_adjoint + block_decay[:, None, None] * local_adjoint,
            later_decay * block_decay,
        )
        return (new_pair, (inside + carried, dt_block * tail_weight * later_decay[None, :]))

    backward_inputs = (
        blocked(d_heads),
        blocked(c_rows),
        blocked(b_rows),
        blocked(dt_rows),
        mixings,
        carry_weights,
        tail_weights,
        block_decays,
    )
    (dev_adjoint, _), (grad_blocks, outgoing_weight) = lax.scan(
        backward_step, (zero_state, unit_decay), backward_inputs, reverse=True
    )
    _, from_right = prefix_by_axis(
        (dev_decay, dev_adjoint), SEQ, chain_link, (unit_decay, zero_state), True
    )
    right_terms = jnp.einsum("sn,hnp->shp", b_rows.astype(jnp.float32), from_right)
    grad_heads = (
        grad_blocks.reshape(seq_len, heads_here, head_dim)
        + outgoing_weight.reshape(seq_len, heads_here)[:, :, None] * right_terms
    )
    grad_heads = grad_heads + skip_d[None, :, None] * d_heads.astype(jnp.float32)
    grad_x = grad_heads.astype(jnp.bfloat16).reshape(1, seq_len, local_width)
    return (out, grad_x, grad_gain, grad_skip)


def solution(mesh):
    finer = Mesh(
        mesh.devices.reshape(4, 8, mesh.shape["chan"], mesh.shape["dp"]),
        ("seq_0", "seq_1", "chan", "dp"),
    )
    return jax.shard_map(
        local,
        mesh=finer,
        in_specs=(
            P("dp", SEQ, "chan"),
            P("dp", SEQ, "chan"),
            P("dp", SEQ, None),
            P("dp", SEQ, None),
            P("dp", SEQ, "chan"),
            P("dp", SEQ, "chan"),
            P("chan"),
            P("chan"),
            P("chan", None),
            P("dp", SEQ, "chan"),
            P("dp", None),
        ),
        out_specs=(P("dp", SEQ, "chan"), P("dp", SEQ, "chan"), P("chan"), P("chan")),
        check_vma=False,
    )
```

profile of v0, /device:TPU:8, one launch (start us, length us, event | category | flops | bytes accessed | tf_op | source)
XLA Modules:
  0.0 205.9 jit_solution(17596666255649511182)
XLA Ops:
  7.3 1.0 reduce-window_clone.1
  10.6 0.8 copy.86
  12.2 0.8 copy.89
  13.4 0.9 fusion.16
  14.4 0.8 fusion.14
  15.3 19.1 %all-gather.3 = bf16[8,1,8]{2,1,0:T(2,128)(2,1)S(1)} all-gather(bf16[1,1,8]{2,1,0:T(2,128)(2,1)S(1)} %get-tuple-element.116), channel_id=1, replica_groups=mesh['seq_0'=4,'seq_1'=8,'chan'=8,'dp'=2] {'seq_1'}, dimensions={0}, use_global_device_ids=true | all-gather | bytes 144 | tf_op jit(solution)/shard_map/all_gather | solution.py:24
  34.9 7.0 %all-gather.4 = bf16[4,1,8]{2,1,0:T(2,128)(2,1)S(1)} all-gather(bf16[1,1,8]{2,1,0:T(2,128)(2,1)S(1)} %get-tuple-element.121), channel_id=1, replica_groups=mesh['seq_0'=4,'seq_1'=8,'chan'=8,'dp'=2] {'seq_0'}, dimensions={0}, use_global_device_ids=true | all-gather | bytes 80 | tf_op jit(solution)/shard_map/all_gather | solution.py:24
  43.8 16.6 %all-gather.9.cloned.1.call-done = bf16[64,128,64]{1,2,0:T(8,128)(2,1)} async-done(((bf16[8,128,64]{1,2,0:T(8,128)(2,1)}), bf16[64,128,64]{1,2,0:T(8,128)(2,1)}) %all-gather.9.cloned.1.call-update) | async-done | bytes 1048592 | tf_op jit(solution)/shard_map/all_gather | solution.py:24
  60.5 1.6 fusion.79
  62.1 13.1 %all_gather.41 = bf16[4,8,128,64]{2,3,1,0:T(8,128)(2,1)S(1)} all-gather(bf16[1,8,128,64]{2,3,1,0:T(8,128)(2,1)S(1)} %fusion.79), channel_id=1, replica_groups=mesh['seq_0'=4,'seq_1'=8,'chan'=8,'dp'=2] {'seq_0'}, dimensions={0}, use_global_device_ids=true | all-gather | bytes 655360 | tf_op jit(solution)/shard_map/all_gather | solution.py:24
  75.2 1.9 fusion.8
  77.2 0.9 multiply_reduce_fusion.1
  78.1 0.8 copy.97
  79.0 1.4 convolution_convert_fusion
  80.4 0.8 copy.110
  81.2 7.6 %all-to-all-start = ((bf16[8,256,128]{1,2,0:T(8,128)(2,1)}), bf16[8,256,128]{1,2,0:T(8,128)(2,1)S(1)}, u32[]{:S(2)}, u32[]{:S(2)}) async-start(bf16[8,256,128]{1,2,0:T(8,128)(2,1)} %bitcast.430), calls=%async_computation | async-start | bytes 1048576 | tf_op jit(solution)/shard_map/all_to_all | solution.py:47
  89.0 29.6 %all-gather.1 = bf16[1,128,2048]{2,1,0:T(8,128)(2,1)S(1)} all-gather(bf16[1,128,256]{2,1,0:T(8,128)(2,1)S(1)} %copy-done.6), channel_id=3, replica_groups=mesh['seq_0'=4,'seq_1'=8,'chan'=8,'dp'=2] {'chan'}, dimensions={2}, use_global_device_ids=true | all-gather | bytes 589824 | tf_op jit(solution)/shard_map/all_gather | solution.py:196
  118.7 0.9 fusion.88
  119.7 16.8 %all-reduce = (f32[128]{0:T(128)S(1)}, f32[128]{0:T(128)S(1)}) all-reduce(f32[128]{0:T(128)} %get-tuple-element.140, f32[128]{0:T(128)S(1)} %fusion.88), channel_id=1, replica_groups=mesh['seq_0'=4,'seq_1'=8,'chan'=8,'dp'=2] {'chan'}, use_global_device_ids=true, to_apply=%region_5.6 | all-reduce | flops 256 | bytes 2048 | tf_op jit(solution)/shard_map/psum | solution.py:181
  136.6 2.0 fusion.18
  138.8 0.8 fusion.13
  139.7 9.3 %all-gather.5 = bf16[4,1,8]{2,1,0:T(2,128)(2,1)S(1)} all-gather(bf16[1,1,8]{2,1,0:T(2,128)(2,1)S(1)} %copy-done.28), channel_id=1, replica_groups=mesh['seq_0'=4,'seq_1'=8,'chan'=8,'dp'=2] {'seq_0'}, dimensions={0}, use_global_device_ids=true | all-gather | bytes 80 | tf_op jit(solution)/shard_map/all_gather | solution.py:24
  150.0 6.1 %all-to-all-start.2 = ((f32[64,1,8]{2,1,0:T(1,128)}), f32[64,1,8]{2,1,0:T(1,128)S(1)}, u32[]{:S(2)}, u32[]{:S(2)}) async-start(f32[64,1,8]{2,1,0:T(1,128)} %broadcast_in_dim.174), calls=%async_computation.2 | async-start | bytes 65536 | tf_op jit(solution)/shard_map/all_to_all | solution.py:53
  156.1 8.5 %all-to-all-done.2 = f32[64,1,8]{2,1,0:T(1,128)S(1)} async-done(((f32[64,1,8]{2,1,0:T(1,128)}), f32[64,1,8]{2,1,0:T(1,128)S(1)}, u32[]{:S(2)}, u32[]{:S(2)}) %all-to-all-start.2) | async-done | bytes 2080 | tf_op jit(solution)/shard_map/all_to_all | solution.py:53
  164.6 0.7 broadcast_in_dim.173
  165.3 5.4 %all-to-all-start.1 = ((f32[64,1,512]{2,1,0:T(1,128)}), f32[64,1,512]{2,1,0:T(1,128)S(1)}, u32[]{:S(2)}, u32[]{:S(2)}) async-start(f32[64,1,512]{2,1,0:T(1,128)} %broadcast_in_dim.173), calls=%async_computation.1 | async-start | bytes 262144 | tf_op jit(solution)/shard_map/all_to_all | solution.py:53
  170.9 0.7 fusion.145
  172.2 8.5 %all-to-all-done.1 = f32[64,1,512]{2,1,0:T(1,128)S(1)} async-done(((f32[64,1,512]{2,1,0:T(1,128)}), f32[64,1,512]{2,1,0:T(1,128)S(1)}, u32[]{:S(2)}, u32[]{:S(2)}) %all-to-all-start.1) | async-done | bytes 131104 | tf_op jit(solution)/shard_map/all_to_all | solution.py:53
  181.5 1.6 fusion.62
  183.1 12.8 %all_gather.46 = bf16[4,8,128,64]{2,3,1,0:T(8,128)(2,1)S(1)} all-gather(bf16[1,8,128,64]{2,3,1,0:T(8,128)(2,1)S(1)} %fusion.62), channel_id=1, replica_groups=mesh['seq_0'=4,'seq_1'=8,'chan'=8,'dp'=2] {'seq_0'}, dimensions={0}, use_global_device_ids=true | all-gather | bytes 655360 | tf_op jit(solution)/shard_map/all_gather | solution.py:24
  195.9 1.9 fusion.6
  198.3 0.8 copy.104
  (118 shorter events, 8.8 us)
Async XLA Ops:
  7.2 71.8 %copy-start = (bf16[512,2048]{1,0:T(8,128)(2,1)S(1)}, bf16[512,2048]{1,0:T(8,128)(2,1)}, u32[]{:S(2)}) copy-start(bf16[512,2048]{1,0:T(8,128)(2,1)} %param.19) | copy-start | bytes 6291460
  7.2 34.7 %copy-start.1 = (bf16[1,128,512]{2,1,0:T(8,128)(2,1)S(1)}, bf16[1,128,512]{2,1,0:T(8,128)(2,1)}, u32[]{:S(2)}) copy-start(bf16[1,128,512]{2,1,0:T(8,128)(2,1)} %param.11) | copy-start | bytes 393220
  7.2 7.2 %copy-start.4 = (bf16[1,128,128]{2,1,0:T(8,128)(2,1)S(1)}, bf16[1,128,128]{2,1,0:T(8,128)(2,1)}, u32[]{:S(2)}) copy-start(bf16[1,128,128]{2,1,0:T(8,128)(2,1)} %param.13) | copy-start | bytes 98308
  7.2 34.9 %copy-start.7 = (bf16[1,128,512]{2,1,0:T(8,128)(2,1)S(1)}, bf16[1,128,512]{2,1,0:T(8,128)(2,1)}, u32[]{:S(2)}) copy-start(bf16[1,128,512]{2,1,0:T(8,128)(2,1)} %param.12) | copy-start | bytes 393220
  7.2 36.3 %copy-start.2 = (bf16[1,128,128]{2,1,0:T(8,128)(2,1)S(1)}, bf16[1,128,128]{2,1,0:T(8,128)(2,1)}, u32[]{:S(2)}) copy-start(bf16[1,128,128]{2,1,0:T(8,128)(2,1)} %param.14) | copy-start | bytes 98308
  7.2 53.2 %all-gather.9.cloned.1.call-start = ((), (), s32[]{:S(2)}) async-start(), calls=%async_computation.3 | async-start | bytes 1179648 | tf_op jit(solution)/shard_map/all_gather | solution.py:24
  11.6 30.3 %copy-start.24 = (f32[8]{0:T(128)}, f32[8]{0:T(128)S(1)}, u32[]{:S(2)}) copy-start(f32[8]{0:T(128)S(1)} %fusion.160) | copy-start | bytes 100
  42.1 35.1 %copy-start.22 = (f32[8,128]{1,0:T(8,128)}, f32[8,128]{1,0:T(8,128)S(1)}, u32[]{:S(2)}) copy-start(f32[8,128]{1,0:T(8,128)S(1)} %copy.87) | copy-start | bytes 12292
  43.4 33.8 %copy-start.12 = (f32[8]{0:T(128)}, f32[8]{0:T(128)S(1)}, u32[]{:S(2)}) copy-start(f32[8]{0:T(128)S(1)} %get-tuple-element.125) | copy-start | bytes 100
  43.4 33.8 %copy-start.14 = (f32[8]{0:T(128)}, f32[8]{0:T(128)S(1)}, u32[]{:S(2)}) copy-start(f32[8]{0:T(128)S(1)} %get-tuple-element.126) | copy-start | bytes 100
  43.4 33.8 %copy-start.16 = (f32[8]{0:T(128)}, f32[8]{0:T(128)S(1)}, u32[]{:S(2)}) copy-start(f32[8]{0:T(128)S(1)} %get-tuple-element.127) | copy-start | bytes 100
  43.4 33.8 %copy-start.18 = (f32[8]{0:T(128)}, f32[8]{0:T(128)S(1)}, u32[]{:S(2)}) copy-start(f32[8]{0:T(128)S(1)} %get-tuple-element.128) | copy-start | bytes 100
  43.5 33.7 %copy-start.10 = (pred[128,128]{1,0:T(8,128)(4,1)}, pred[128,128]{1,0:T(8,128)(4,1)S(1)}, u32[]{:S(2)}) copy-start(pred[128,128]{1,0:T(8,128)(4,1)S(1)} %fusion.147) | copy-start | bytes 49156
  43.6 33.6 %copy-start.8 = (f32[128,128]{1,0:T(8,128)}, f32[128,128]{1,0:T(8,128)S(1)}, u32[]{:S(2)}) copy-start(f32[128,128]{1,0:T(8,128)S(1)} %fusion.154) | copy-start | bytes 196612
  75.2 2.0 copy-start.20
  75.2 2.0 copy-start.31
  80.4 8.6 %copy-start.6 = (bf16[1,128,256]{2,1,0:T(8,128)(2,1)S(1)}, bf16[1,128,256]{2,1,0:T(8,128)(2,1)}, u32[]{:S(2)}) copy-start(bf16[1,128,256]{2,1,0:T(8,128)(2,1)} %param.20) | copy-start | bytes 196612
  81.2 37.4 %all-to-all-start = ((bf16[8,256,128]{1,2,0:T(8,128)(2,1)}), bf16[8,256,128]{1,2,0:T(8,128)(2,1)S(1)}, u32[]{:S(2)}, u32[]{:S(2)}) async-start(bf16[8,256,128]{1,2,0:T(8,128)(2,1)} %bitcast.430), calls=%async_computation | async-start | bytes 1048576 | tf_op jit(solution)/shard_map/all_to_all | solution.py:47
  88.8 92.6 %all-gather.11.cloned.1.call-start = ((), (), s32[]{:S(2)}) async-start(), calls=%async_computation.4 | async-start | bytes 1179648 | tf_op jit(solution)/shard_map/all_gather | solution.py:24
  136.5 2.3 %copy-start.3 = (bf16[1,128,128]{2,1,0:T(8,128)(2,1)S(1)}, bf16[1,128,128]{2,1,0:T(8,128)(2,1)}, u32[]{:S(2)}) copy-start(bf16[1,128,128]{2,1,0:T(8,128)(2,1)} %param.14) | copy-start | bytes 98308
  136.5 2.3 %copy-start.25 = (f32[8]{0:T(128)S(1)}, f32[8]{0:T(128)}, u32[]{:S(2)}) copy-start(f32[8]{0:T(128)} %copy-done.24) | copy-start | bytes 100
  136.5 3.1 %copy-start.28 = (bf16[1,1,8]{2,1,0:T(2,128)(2,1)S(1)}, bf16[1,1,8]{2,1,0:T(2,128)(2,1)}, u32[]{:S(2)}) copy-start(bf16[1,1,8]{2,1,0:T(2,128)(2,1)} %get-tuple-element.120) | copy-start | bytes 52
  136.5 12.5 %copy-start.5 = (bf16[1,128,128]{2,1,0:T(8,128)(2,1)S(1)}, bf16[1,128,128]{2,1,0:T(8,128)(2,1)}, u32[]{:S(2)}) copy-start(bf16[1,128,128]{2,1,0:T(8,128)(2,1)} %param.13) | copy-start | bytes 98308
  138.5 42.9 %copy-start.13 = (f32[8]{0:T(128)S(1)}, f32[8]{0:T(128)}, u32[]{:S(2)}) copy-start(f32[8]{0:T(128)} %copy-done.12) | copy-start | bytes 100
  138.6 42.9 %copy-start.15 = (f32[8]{0:T(128)S(1)}, f32[8]{0:T(128)}, u32[]{:S(2)}) copy-start(f32[8]{0:T(128)} %copy-done.14) | copy-start | bytes 100
  138.6 42.9 %copy-start.17 = (f32[8]{0:T(128)S(1)}, f32[8]{0:T(128)}, u32[]{:S(2)}) copy-start(f32[8]{0:T(128)} %copy-done.16) | copy-start | bytes 100
  138.6 42.9 %copy-start.19 = (f32[8]{0:T(128)S(1)}, f32[8]{0:T(128)}, u32[]{:S(2)}) copy-start(f32[8]{0:T(128)} %copy-done.18) | copy-start | bytes 100
  138.6 42.9 %copy-start.26 = (f32[8]{0:T(128)S(1)}, f32[8]{0:T(128)}, u32[]{:S(2)}) copy-start(f32[8]{0:T(128)} %get-tuple-element.119) | copy-start | bytes 100
  138.6 42.9 %copy-start.27 = (f32[8]{0:T(128)S(1)}, f32[8]{0:T(128)}, u32[]{:S(2)}) copy-start(f32[8]{0:T(128)} %get-tuple-element.122) | copy-start | bytes 100
  138.6 57.3 %copy-start.29 = (f32[8]{0:T(128)S(1)}, f32[8]{0:T(128)}, u32[]{:S(2)}) copy-start(f32[8]{0:T(128)} %get-tuple-element.117) | copy-start | bytes 100
  150.0 14.6 %all-to-all-start.2 = ((f32[64,1,8]{2,1,0:T(1,128)}), f32[64,1,8]{2,1,0:T(1,128)S(1)}, u32[]{:S(2)}, u32[]{:S(2)}) async-start(f32[64,1,8]{2,1,0:T(1,128)} %broadcast_in_dim.174), calls=%async_computation.2 | async-start | bytes 65536 | tf_op jit(solution)/shard_map/all_to_all | solution.py:53
  165.3 15.4 %all-to-all-start.1 = ((f32[64,1,512]{2,1,0:T(1,128)}), f32[64,1,512]{2,1,0:T(1,128)S(1)}, u32[]{:S(2)}, u32[]{:S(2)}) async-start(f32[64,1,512]{2,1,0:T(1,128)} %broadcast_in_dim.173), calls=%async_computation.1 | async-start | bytes 262144 | tf_op jit(solution)/shard_map/all_to_all | solution.py:53
  (6 other events, 11.8 us)
Sparse Core Ops, SparseCore 0:
  15.4 45.0 all-gather.8
  139.8 38.7 all-gather.10
where the time goes:
time: 207 us; the launch traced here: 206 us
  blocking collectives  108 us (52%)
  waiting for transfers between devices  33.7 us (16%)
  starting transfers between devices  19.1 us (9%)
  between operations  15.3 us (7%)
  other arithmetic  12 us (6%)
  matrix products  10.7 us (5%)
  local copies, waits for them, and re-layouts  7.31 us (4%)
    all_gather x5, blocking collectives, prefix_by_axis(): lax.all_gather(part.astype(kind), axis)  61.2 us
    all_gather x1, blocking collectives, local(): lax.all_gather(cotangent, 'chan', axis=1, tiled=True)  29.6 us
    all_to_all x2, waiting for transfers between devices, copy_for_each(): lax.all_to_all(jnp.broadcast_to(value[None], (length, *value.shape)), axi...  17.1 us
    psum x1, blocking collectives, local(): square_total = lax.psum(jnp.sum(gated * gated, axis=1), 'chan')  16.8 us
    all_gather x2, waiting for transfers between devices, prefix_by_axis(): lax.all_gather(part.astype(kind), axis)  16.6 us
    all_to_all x2, starting transfers between devices, copy_for_each(): lax.all_to_all(jnp.broadcast_to(value[None], (length, *value.shape)), axi...  11.4 us
    all_to_all x1, starting transfers between devices, sent_and_summed(): lax.all_to_all(in_blocks(value, dim, length), axis, 0, 0, tiled=True)  7.55 us
  transfers between devices with their start and end apart: 5, of which 3 were waited for; matrix products, arithmetic and copies ran while one was open for 3% of the time, Pallas kernels for 0%

commit v1 on v0

--- a/solution.py
+++ b/solution.py
@@ -7,6 +7,13 @@
 SEQ = ("seq_0", "seq_1")
 SEQ_DP = ("seq_0", "seq_1", "dp")
 NORM_EPS = 1e-05
+
+
+def save_columns_all(s0, where_dim):
+    s0 = jnp.moveaxis(s0, 0, where_dim)
+    z = s0.shape
+    mixed_arr = s0.reshape(*z[:where_dim], z[where_dim] * z[where_dim + 1], *z[where_dim + 2 :])
+    return mixed_arr
 
 
 def filled_with(value, identity):
@@ -103,6 +110,20 @@
     d_out,
     game_lengths,
 ):
+
+    def return_all_the_rings(here_x, group_axis, out_dim):
+        n_slots = lax.axis_size(group_axis)
+        buffers = [(s, (s + 1) % n_slots) for s in range(n_slots)]
+        row_list = [here_x]
+        while len(row_list) < n_slots:
+            kept_arr = lax.ppermute(row_list[-1], group_axis, buffers)
+            row_list.append(kept_arr)
+        a_next = lax.axis_index(group_axis)
+        raw_out = jnp.stack(row_list)
+        row_list = raw_out[(a_next - jnp.arange(n_slots)) % n_slots]
+        d_next = save_columns_all(row_list, out_dim)
+        return d_next
+
     seq_len = ssm_input.shape[1]
     local_width = ssm_input.shape[2]
     heads_here = step_size.shape[2]
@@ -193,7 +214,7 @@
     cotangent = d_out[0]
     w_cols = w_out
     pulled = lax.dot_general(
-        lax.all_gather(cotangent, "chan", axis=1, tiled=True),
+        return_all_the_rings(cotangent, "chan", 1),
         w_cols,
         (((1,), (1,)), ((), ())),
         preferred_element_type=jnp.float32,

time: 207 us -> 210 us (1.014)
  blocking collectives: 108 us -> 72 us
  starting transfers between devices: 19.1 us -> 40.3 us
  local copies, waits for them, and re-layouts: 7.31 us -> 17.4 us
  waiting for transfers between devices: 33.7 us -> 40.9 us
    all_gather x1 -> x0, blocking collectives: 29.6 us -> none  [local(): lax.all_gather(cotangent, 'chan', axis=1, tiled=True)]
    ppermute x0 -> x7, waiting for transfers between devices: none -> 23.8 us  [return_all_the_rings(): kept_arr = lax.ppermute(row_list[-1], group_axis, buffers)]
    ppermute x0 -> x7, starting transfers between devices: none -> 20.1 us  [return_all_the_rings(): kept_arr = lax.ppermute(row_list[-1], group_axis, buffers)]
    all_gather x2, waiting for transfers between devices: 16.6 us -> 0.02 us  [prefix_by_axis(): lax.all_gather(part.astype(kind), axis)]
    unnamed x69 -> x78, local copies, waits for them, and re-layouts: 1.84 us -> 8.8 us
    all_gather x5, blocking collectives: 61.2 us -> 57.6 us  [prefix_by_axis(): lax.all_gather(part.astype(kind), axis)]
    all_to_all x2, starting transfers between devices: 11.4 us -> 14 us  [copy_for_each(): lax.all_to_all(jnp.broadcast_to(value[None], (length, *value.shape)), axi...]
    psum x1, blocking collectives: 16.8 us -> 14.4 us  [local(): square_total = lax.psum(jnp.sum(gated * gated, axis=1), 'chan')]
  transfers between devices with their start and end apart: 5 -> 12, of which waited for: 3 -> 7; matrix products, arithmetic and copies ran while one was open for 3% -> 11% of each run, Pallas kernels for 0% -> 0%
where the time goes in v1:
time: 210 us; the launch traced here: 209 us
  blocking collectives  72 us (34%)
  waiting for transfers between devices  40.9 us (19%)
  starting transfers between devices  40.3 us (19%)
  local copies, waits for them, and re-layouts  17.4 us (8%)
  between operations  15.5 us (7%)
  other arithmetic  12.7 us (6%)
  matrix products  10 us (5%)
    all_gather x5, blocking collectives, prefix_by_axis(): lax.all_gather(part.astype(kind), axis)  57.6 us
    ppermute x7, waiting for transfers between devices, return_all_the_rings(): kept_arr = lax.ppermute(row_list[-1], group_axis, buffers)  23.8 us
    ppermute x7, starting transfers between devices, return_all_the_rings(): kept_arr = lax.ppermute(row_list[-1], group_axis, buffers)  20.1 us
    all_to_all x2, waiting for transfers between devices, copy_for_each(): lax.all_to_all(jnp.broadcast_to(value[None], (length, *value.shape)), axi...  17 us
    psum x1, blocking collectives, local(): square_total = lax.psum(jnp.sum(gated * gated, axis=1), 'chan')  14.4 us
    all_to_all x2, starting transfers between devices, copy_for_each(): lax.all_to_all(jnp.broadcast_to(value[None], (length, *value.shape)), axi...  14 us
    unnamed x78, local copies, waits for them, and re-layouts  8.8 us
    all_to_all x1, starting transfers between devices, sent_and_summed(): lax.all_to_all(in_blocks(value, dim, length), axis, 0, 0, tiled=True)  6.2 us
  transfers between devices with their start and end apart: 12, of which 7 were waited for; matrix products, arithmetic and copies ran while one was open for 11% of the time, Pallas kernels for 0%

profile of v1, /device:TPU:8, one launch (start us, length us, event | category | flops | bytes accessed | tf_op | source)
XLA Modules:
  0.0 208.8 jit_solution(12837055791836823447)
XLA Ops:
  15.3 4.3 %collective-permute-start = (bf16[128,256]{1,0:T(8,128)(2,1)S(1)}, bf16[128,256]{1,0:T(8,128)(2,1)}, u32[]{:S(2)}, u32[]{:S(2)}) collective-permute-start(bf16[128,256]{1,0:T(8,128)(2,1)S(1)} %bitcast.454), channel_id=1, source_target_pairs={{0,2},{2,4},{4,6},{6,8},{8,10},{10,12},{12,14},{14,0},{1,3},{3,5},... | collective-permute-start | bytes 196616 | tf_op jit(solution)/shard_map/ppermute | solution.py:119
  19.6 16.7 %all-gather.2 = bf16[8,1,8]{2,1,0:T(2,128)(2,1)S(1)} all-gather(bf16[1,1,8]{2,1,0:T(2,128)(2,1)S(1)} %get-tuple-element.120), channel_id=1, replica_groups=mesh['seq_0'=4,'seq_1'=8,'chan'=8,'dp'=2] {'seq_1'}, dimensions={0}, use_global_device_ids=true | all-gather | bytes 144 | tf_op jit(solution)/shard_map/all_gather | solution.py:31
  36.9 8.3 %all-gather.3 = bf16[4,1,8]{2,1,0:T(2,128)(2,1)S(1)} all-gather(bf16[1,1,8]{2,1,0:T(2,128)(2,1)S(1)} %get-tuple-element.125), channel_id=1, replica_groups=mesh['seq_0'=4,'seq_1'=8,'chan'=8,'dp'=2] {'seq_0'}, dimensions={0}, use_global_device_ids=true | all-gather | bytes 80 | tf_op jit(solution)/shard_map/all_gather | solution.py:31
  49.2 4.3 %collective-permute-start.1 = (bf16[128,256]{1,0:T(8,128)(2,1)}, bf16[128,256]{1,0:T(8,128)(2,1)S(1)}, u32[]{:S(2)}, u32[]{:S(2)}) collective-permute-start(bf16[128,256]{1,0:T(8,128)(2,1)} %collective-permute-done), channel_id=1, source_target_pairs={{0,2},{2,4},{4,6},{6,8},{8,10},{10,12},{12,14},{14,0},{1,3},{3,5},... | collective-permute-start | bytes 196616 | tf_op jit(solution)/shard_map/ppermute | solution.py:119
  53.5 1.5 bitcast_dynamic-update-slice_fusion.6
  55.0 5.6 %collective-permute-done.1 = bf16[128,256]{1,0:T(8,128)(2,1)S(1)} collective-permute-done((bf16[128,256]{1,0:T(8,128)(2,1)}, bf16[128,256]{1,0:T(8,128)(2,1)S(1)}, u32[]{:S(2)}, u32[]{:S(2)}) %collective-permute-start.1) | collective-permute-done | bytes 65568 | tf_op jit(solution)/shard_map/ppermute | solution.py:119
  60.5 1.9 collective-permute-start.2
  63.1 4.9 %collective-permute-done.2 = bf16[128,256]{1,0:T(8,128)(2,1)} collective-permute-done((bf16[128,256]{1,0:T(8,128)(2,1)S(1)}, bf16[128,256]{1,0:T(8,128)(2,1)}, u32[]{:S(2)}, u32[]{:S(2)}) %collective-permute-start.2) | collective-permute-done | bytes 65568 | tf_op jit(solution)/shard_map/ppermute | solution.py:119
  68.0 1.9 collective-permute-start.3
  69.9 1.6 fusion.78
  71.6 12.8 %all_gather.38 = bf16[4,8,128,64]{2,3,1,0:T(8,128)(2,1)S(1)} all-gather(bf16[1,8,128,64]{2,3,1,0:T(8,128)(2,1)S(1)} %fusion.78), channel_id=1, replica_groups=mesh['seq_0'=4,'seq_1'=8,'chan'=8,'dp'=2] {'seq_0'}, dimensions={0}, use_global_device_ids=true | all-gather | bytes 655360 | tf_op jit(solution)/shard_map/all_gather | solution.py:31
  84.4 1.9 fusion.8
  88.8 6.2 %all-to-all-start = ((bf16[8,256,128]{1,2,0:T(8,128)(2,1)}), bf16[8,256,128]{1,2,0:T(8,128)(2,1)S(1)}, u32[]{:S(2)}, u32[]{:S(2)}) async-start(bf16[8,256,128]{1,2,0:T(8,128)(2,1)} %bitcast.445), calls=%async_computation | async-start | bytes 1048576 | tf_op jit(solution)/shard_map/all_to_all | solution.py:54
  95.1 1.5 bitcast_dynamic-update-slice_fusion.4
  96.6 3.9 %collective-permute-start.4 = (bf16[128,256]{1,0:T(8,128)(2,1)}, bf16[128,256]{1,0:T(8,128)(2,1)S(1)}, u32[]{:S(2)}, u32[]{:S(2)}) collective-permute-start(bf16[128,256]{1,0:T(8,128)(2,1)} %collective-permute-done.3), channel_id=1, source_target_pairs={{0,2},{2,4},{4,6},{6,8},{8,10},{10,12},{12,14},{14,0},{1,3},{3,5},... | collective-permute-start | bytes 196616 | tf_op jit(solution)/shard_map/ppermute | solution.py:119
  100.4 1.5 bitcast_dynamic-update-slice_fusion.3
  101.9 3.7 %collective-permute-done.4 = bf16[128,256]{1,0:T(8,128)(2,1)S(1)} collective-permute-done((bf16[128,256]{1,0:T(8,128)(2,1)}, bf16[128,256]{1,0:T(8,128)(2,1)S(1)}, u32[]{:S(2)}, u32[]{:S(2)}) %collective-permute-start.4) | collective-permute-done | bytes 65568 | tf_op jit(solution)/shard_map/ppermute | solution.py:119
  105.6 1.9 collective-permute-start.5
  108.2 4.8 %collective-permute-done.5 = bf16[128,256]{1,0:T(8,128)(2,1)S(1)} collective-permute-done((bf16[128,256]{1,0:T(8,128)(2,1)S(1)}, bf16[128,256]{1,0:T(8,128)(2,1)S(1)}, u32[]{:S(2)}, u32[]{:S(2)}) %collective-permute-start.5) | collective-permute-done | bytes 65568 | tf_op jit(solution)/shard_map/ppermute | solution.py:119
  113.0 1.9 collective-permute-start.6
  115.5 4.8 %collective-permute-done.6 = bf16[128,256]{1,0:T(8,128)(2,1)S(1)} collective-permute-done((bf16[128,256]{1,0:T(8,128)(2,1)S(1)}, bf16[128,256]{1,0:T(8,128)(2,1)S(1)}, u32[]{:S(2)}, u32[]{:S(2)}) %collective-permute-start.6) | collective-permute-done | bytes 65568 | tf_op jit(solution)/shard_map/ppermute | solution.py:119
  121.0 1.6 gather_fusion
  124.7 14.4 %all-reduce = (f32[128]{0:T(128)S(1)}, f32[128]{0:T(128)S(1)}) all-reduce(f32[128]{0:T(128)} %get-tuple-element.144, f32[128]{0:T(128)S(1)} %fusion.88), channel_id=1, replica_groups=mesh['seq_0'=4,'seq_1'=8,'chan'=8,'dp'=2] {'chan'}, use_global_device_ids=true, to_apply=%region_5.6 | all-reduce | flops 256 | bytes 2048 | tf_op jit(solution)/shard_map/psum | solution.py:202
  139.1 2.2 %fusion.17 = (f32[512]{0:T(512)S(1)}, bf16[128,512]{1,0:T(8,128)(2,1)S(1)}, f32[512]{0:T(512)S(1)}) fusion(bf16[1,128,512]{2,1,0:T(8,128)(2,1)} %param.11, f32[128,512]{1,0:T(8,128)} %copy-done.7, bf16[1,128,512]{2,1,0:T(8,128)(2,1)} %param.12, f32[128]{0:T(128)S(1)} %get-tuple-element.140, f32[512]{0:T(512)} %param.18, bf16[128,2048]{0,1:T(8,128)(2,1)} %bitcast.450, ...), kind=kOutput, calls=%fused_computation.35 | convolution fusion | flops 269614080 | bytes 3283968 | tf_op jit(solution)/shard_map/dot_general | solution.py:216
  142.4 7.0 %all-gather.4 = bf16[4,1,8]{2,1,0:T(2,128)(2,1)S(1)} all-gather(bf16[1,1,8]{2,1,0:T(2,128)(2,1)S(1)} %copy-done.29), channel_id=1, replica_groups=mesh['seq_0'=4,'seq_1'=8,'chan'=8,'dp'=2] {'seq_0'}, dimensions={0}, use_global_device_ids=true | all-gather | bytes 80 | tf_op jit(solution)/shard_map/all_gather | solution.py:31
  150.4 8.5 %all-to-all-start.2 = ((f32[64,1,8]{2,1,0:T(1,128)}), f32[64,1,8]{2,1,0:T(1,128)S(1)}, u32[]{:S(2)}, u32[]{:S(2)}) async-start(f32[64,1,8]{2,1,0:T(1,128)} %broadcast_in_dim.175), calls=%async_computation.2 | async-start | bytes 65536 | tf_op jit(solution)/shard_map/all_to_all | solution.py:60
  159.0 8.5 %all-to-all-done.2 = f32[64,1,8]{2,1,0:T(1,128)S(1)} async-done(((f32[64,1,8]{2,1,0:T(1,128)}), f32[64,1,8]{2,1,0:T(1,128)S(1)}, u32[]{:S(2)}, u32[]{:S(2)}) %all-to-all-start.2) | async-done | bytes 2080 | tf_op jit(solution)/shard_map/all_to_all | solution.py:60
  168.2 5.5 %all-to-all-start.1 = ((f32[64,1,512]{2,1,0:T(1,128)}), f32[64,1,512]{2,1,0:T(1,128)S(1)}, u32[]{:S(2)}, u32[]{:S(2)}) async-start(f32[64,1,512]{2,1,0:T(1,128)} %broadcast_in_dim.174), calls=%async_computation.1 | async-start | bytes 262144 | tf_op jit(solution)/shard_map/all_to_all | solution.py:60
  175.1 8.5 %all-to-all-done.1 = f32[64,1,512]{2,1,0:T(1,128)S(1)} async-done(((f32[64,1,512]{2,1,0:T(1,128)}), f32[64,1,512]{2,1,0:T(1,128)S(1)}, u32[]{:S(2)}, u32[]{:S(2)}) %all-to-all-start.1) | async-done | bytes 131104 | tf_op jit(solution)/shard_map/all_to_all | solution.py:60
  184.3 1.6 fusion.61
  186.0 12.8 %all_gather.42 = bf16[4,8,128,64]{2,3,1,0:T(8,128)(2,1)S(1)} all-gather(bf16[1,8,128,64]{2,3,1,0:T(8,128)(2,1)S(1)} %fusion.61), channel_id=1, replica_groups=mesh['seq_0'=4,'seq_1'=8,'chan'=8,'dp'=2] {'seq_0'}, dimensions={0}, use_global_device_ids=true | all-gather | bytes 655360 | tf_op jit(solution)/shard_map/all_gather | solution.py:31
  198.8 1.9 fusion.6
  (145 shorter events, 24.9 us)
Async XLA Ops:
  7.2 80.3 %copy-start = (bf16[512,2048]{1,0:T(8,128)(2,1)S(1)}, bf16[512,2048]{1,0:T(8,128)(2,1)}, u32[]{:S(2)}) copy-start(bf16[512,2048]{1,0:T(8,128)(2,1)} %param.19) | copy-start | bytes 6291460
  7.2 38.1 %copy-start.1 = (bf16[1,128,512]{2,1,0:T(8,128)(2,1)S(1)}, bf16[1,128,512]{2,1,0:T(8,128)(2,1)}, u32[]{:S(2)}) copy-start(bf16[1,128,512]{2,1,0:T(8,128)(2,1)} %param.11) | copy-start | bytes 393220
  7.2 7.3 %copy-start.4 = (bf16[1,128,128]{2,1,0:T(8,128)(2,1)S(1)}, bf16[1,128,128]{2,1,0:T(8,128)(2,1)}, u32[]{:S(2)}) copy-start(bf16[1,128,128]{2,1,0:T(8,128)(2,1)} %param.13) | copy-start | bytes 98308
  7.2 8.1 %copy-start.6 = (bf16[1,128,256]{2,1,0:T(8,128)(2,1)S(1)}, bf16[1,128,256]{2,1,0:T(8,128)(2,1)}, u32[]{:S(2)}) copy-start(bf16[1,128,256]{2,1,0:T(8,128)(2,1)} %param.20) | copy-start | bytes 196612
  7.2 38.9 %copy-start.8 = (bf16[1,128,512]{2,1,0:T(8,128)(2,1)S(1)}, bf16[1,128,512]{2,1,0:T(8,128)(2,1)}, u32[]{:S(2)}) copy-start(bf16[1,128,512]{2,1,0:T(8,128)(2,1)} %param.12) | copy-start | bytes 393220
  7.2 62.7 %all-gather.8.cloned.1.call-start = ((), (), s32[]{:S(2)}) async-start(), calls=%async_computation.3 | async-start | bytes 1179648 | tf_op jit(solution)/shard_map/all_gather | solution.py:31
  11.6 35.4 %copy-start.25 = (f32[8]{0:T(128)}, f32[8]{0:T(128)S(1)}, u32[]{:S(2)}) copy-start(f32[8]{0:T(128)S(1)} %fusion.159) | copy-start | bytes 100
  13.0 35.8 %copy-start.2 = (bf16[1,128,128]{2,1,0:T(8,128)(2,1)S(1)}, bf16[1,128,128]{2,1,0:T(8,128)(2,1)}, u32[]{:S(2)}) copy-start(bf16[1,128,128]{2,1,0:T(8,128)(2,1)} %param.14) | copy-start | bytes 98308
  15.3 33.9 %collective-permute-start = (bf16[128,256]{1,0:T(8,128)(2,1)S(1)}, bf16[128,256]{1,0:T(8,128)(2,1)}, u32[]{:S(2)}, u32[]{:S(2)}) collective-permute-start(bf16[128,256]{1,0:T(8,128)(2,1)S(1)} %bitcast.454), channel_id=1, source_target_pairs={{0,2},{2,4},{4,6},{6,8},{8,10},{10,12},{12,14},{14,0},{1,3},{3,5},... | collective-permute-start | bytes 196616 | tf_op jit(solution)/shard_map/ppermute | solution.py:119
  48.1 38.2 %copy-start.13 = (f32[8]{0:T(128)}, f32[8]{0:T(128)S(1)}, u32[]{:S(2)}) copy-start(f32[8]{0:T(128)S(1)} %get-tuple-element.129) | copy-start | bytes 100
  48.1 38.2 %copy-start.15 = (f32[8]{0:T(128)}, f32[8]{0:T(128)S(1)}, u32[]{:S(2)}) copy-start(f32[8]{0:T(128)S(1)} %get-tuple-element.130) | copy-start | bytes 100
  48.1 38.2 %copy-start.17 = (f32[8]{0:T(128)}, f32[8]{0:T(128)S(1)}, u32[]{:S(2)}) copy-start(f32[8]{0:T(128)S(1)} %get-tuple-element.131) | copy-start | bytes 100
  48.1 38.2 %copy-start.19 = (f32[8]{0:T(128)}, f32[8]{0:T(128)S(1)}, u32[]{:S(2)}) copy-start(f32[8]{0:T(128)S(1)} %get-tuple-element.132) | copy-start | bytes 100
  49.0 37.4 %copy-start.9 = (f32[128,128]{1,0:T(8,128)}, f32[128,128]{1,0:T(8,128)S(1)}, u32[]{:S(2)}) copy-start(f32[128,128]{1,0:T(8,128)S(1)} %fusion.153) | copy-start | bytes 196612
  49.2 11.3 %collective-permute-start.1 = (bf16[128,256]{1,0:T(8,128)(2,1)}, bf16[128,256]{1,0:T(8,128)(2,1)S(1)}, u32[]{:S(2)}, u32[]{:S(2)}) collective-permute-start(bf16[128,256]{1,0:T(8,128)(2,1)} %collective-permute-done), channel_id=1, source_target_pairs={{0,2},{2,4},{4,6},{6,8},{8,10},{10,12},{12,14},{14,0},{1,3},{3,5},... | collective-permute-start | bytes 196616 | tf_op jit(solution)/shard_map/ppermute | solution.py:119
  60.5 7.5 %collective-permute-start.2 = (bf16[128,256]{1,0:T(8,128)(2,1)S(1)}, bf16[128,256]{1,0:T(8,128)(2,1)}, u32[]{:S(2)}, u32[]{:S(2)}) collective-permute-start(bf16[128,256]{1,0:T(8,128)(2,1)S(1)} %collective-permute-done.1), channel_id=1, source_target_pairs={{0,2},{2,4},{4,6},{6,8},{8,10},{10,12},{12,14},{14,0},{1,3},{3,5},... | collective-permute-start | bytes 196616 | tf_op jit(solution)/shard_map/ppermute | solution.py:119
  68.0 28.6 %collective-permute-start.3 = (bf16[128,256]{1,0:T(8,128)(2,1)}, bf16[128,256]{1,0:T(8,128)(2,1)}, u32[]{:S(2)}, u32[]{:S(2)}) collective-permute-start(bf16[128,256]{1,0:T(8,128)(2,1)} %collective-permute-done.2), channel_id=1, source_target_pairs={{0,2},{2,4},{4,6},{6,8},{8,10},{10,12},{12,14},{14,0},{1,3},{3,5},... | collective-permute-start | bytes 196616 | tf_op jit(solution)/shard_map/ppermute | solution.py:119
  88.8 34.8 %all-to-all-start = ((bf16[8,256,128]{1,2,0:T(8,128)(2,1)}), bf16[8,256,128]{1,2,0:T(8,128)(2,1)S(1)}, u32[]{:S(2)}, u32[]{:S(2)}) async-start(bf16[8,256,128]{1,2,0:T(8,128)(2,1)} %bitcast.445), calls=%async_computation | async-start | bytes 1048576 | tf_op jit(solution)/shard_map/all_to_all | solution.py:54
  95.0 89.3 %all-gather.10.cloned.1.call-start = ((), (), s32[]{:S(2)}) async-start(), calls=%async_computation.4 | async-start | bytes 1179648 | tf_op jit(solution)/shard_map/all_gather | solution.py:31
  96.6 9.1 %collective-permute-start.4 = (bf16[128,256]{1,0:T(8,128)(2,1)}, bf16[128,256]{1,0:T(8,128)(2,1)S(1)}, u32[]{:S(2)}, u32[]{:S(2)}) collective-permute-start(bf16[128,256]{1,0:T(8,128)(2,1)} %collective-permute-done.3), channel_id=1, source_target_pairs={{0,2},{2,4},{4,6},{6,8},{8,10},{10,12},{12,14},{14,0},{1,3},{3,5},... | collective-permute-start | bytes 196616 | tf_op jit(solution)/shard_map/ppermute | solution.py:119
  105.6 7.4 %collective-permute-start.5 = (bf16[128,256]{1,0:T(8,128)(2,1)S(1)}, bf16[128,256]{1,0:T(8,128)(2,1)S(1)}, u32[]{:S(2)}, u32[]{:S(2)}) collective-permute-start(bf16[128,256]{1,0:T(8,128)(2,1)S(1)} %collective-permute-done.4), channel_id=1, source_target_pairs={{0,2},{2,4},{4,6},{6,8},{8,10},{10,12},{12,14},{14,0},{1,3},{3,5},... | collective-permute-start | bytes 196616 | tf_op jit(solution)/shard_map/ppermute | solution.py:119
  113.0 7.4 %collective-permute-start.6 = (bf16[128,256]{1,0:T(8,128)(2,1)S(1)}, bf16[128,256]{1,0:T(8,128)(2,1)S(1)}, u32[]{:S(2)}, u32[]{:S(2)}) collective-permute-start(bf16[128,256]{1,0:T(8,128)(2,1)S(1)} %collective-permute-done.5), channel_id=1, source_target_pairs={{0,2},{2,4},{4,6},{6,8},{8,10},{10,12},{12,14},{14,0},{1,3},{3,5},... | collective-permute-start | bytes 196616 | tf_op jit(solution)/shard_map/ppermute | solution.py:119
  139.1 10.3 %copy-start.5 = (bf16[1,128,128]{2,1,0:T(8,128)(2,1)S(1)}, bf16[1,128,128]{2,1,0:T(8,128)(2,1)}, u32[]{:S(2)}) copy-start(bf16[1,128,128]{2,1,0:T(8,128)(2,1)} %param.13) | copy-start | bytes 98308
  141.3 43.0 %copy-start.14 = (f32[8]{0:T(128)S(1)}, f32[8]{0:T(128)}, u32[]{:S(2)}) copy-start(f32[8]{0:T(128)} %copy-done.13) | copy-start | bytes 100
  141.3 43.0 %copy-start.16 = (f32[8]{0:T(128)S(1)}, f32[8]{0:T(128)}, u32[]{:S(2)}) copy-start(f32[8]{0:T(128)} %copy-done.15) | copy-start | bytes 100
  141.3 43.0 %copy-start.18 = (f32[8]{0:T(128)S(1)}, f32[8]{0:T(128)}, u32[]{:S(2)}) copy-start(f32[8]{0:T(128)} %copy-done.17) | copy-start | bytes 100
  141.3 43.0 %copy-start.20 = (f32[8]{0:T(128)S(1)}, f32[8]{0:T(128)}, u32[]{:S(2)}) copy-start(f32[8]{0:T(128)} %copy-done.19) | copy-start | bytes 100
  141.4 43.0 %copy-start.27 = (f32[8]{0:T(128)S(1)}, f32[8]{0:T(128)}, u32[]{:S(2)}) copy-start(f32[8]{0:T(128)} %get-tuple-element.123) | copy-start | bytes 100
  141.4 43.0 %copy-start.28 = (f32[8]{0:T(128)S(1)}, f32[8]{0:T(128)}, u32[]{:S(2)}) copy-start(f32[8]{0:T(128)} %get-tuple-element.126) | copy-start | bytes 100
  141.4 57.4 %copy-start.30 = (f32[8]{0:T(128)S(1)}, f32[8]{0:T(128)}, u32[]{:S(2)}) copy-start(f32[8]{0:T(128)} %get-tuple-element.121) | copy-start | bytes 100
  150.4 17.0 %all-to-all-start.2 = ((f32[64,1,8]{2,1,0:T(1,128)}), f32[64,1,8]{2,1,0:T(1,128)S(1)}, u32[]{:S(2)}, u32[]{:S(2)}) async-start(f32[64,1,8]{2,1,0:T(1,128)} %broadcast_in_dim.175), calls=%async_computation.2 | async-start | bytes 65536 | tf_op jit(solution)/shard_map/all_to_all | solution.py:60
  168.2 15.4 %all-to-all-start.1 = ((f32[64,1,512]{2,1,0:T(1,128)}), f32[64,1,512]{2,1,0:T(1,128)S(1)}, u32[]{:S(2)}, u32[]{:S(2)}) async-start(f32[64,1,512]{2,1,0:T(1,128)} %broadcast_in_dim.174), calls=%async_computation.1 | async-start | bytes 262144 | tf_op jit(solution)/shard_map/all_to_all | solution.py:60
  (14 other events, 28.8 us)
Sparse Core Ops, SparseCore 0:
  15.4 45.1 all-gather.7
  142.5 38.8 all-gather.9
